TPU v7x, 8 devices: a whole 2x2x1 slice. The times are simulated.
8 devices in a mesh: dp: 2 (over y, z), tp: 4 (over x, core).
Axes of the slice: x: 2, y: 2, z: 1, core: 2. Of those that a mesh axis runs over, the one named last changes fastest.
Arguments:
- x: bfloat16 [2048, 4096], P(('dp', 'tp')), parts along dimension 0
- w_gate: bfloat16 [4096, 16384], P(None, 'tp')
- w_up: bfloat16 [4096, 16384], P(None, 'tp')
- w_down: bfloat16 [16384, 4096], P('tp')
Outputs:
- output: bfloat16 [2048, 4096], P(('dp', 'tp')), parts along dimension 0
There are 2 independent parts. A program takes and returns all parts, laid end to end along the dimension named above; an argument that names none is the same for every part.
All inputs are finite; a program needn't handle non-finite values.
Results may differ from a plain program's by a relative error of at most 0.016.
Values are sent between devices in bfloat16 or wider.
A program may use at most 2 GiB of HBM per device.

v0:
```python
import jax
import jax.numpy as jnp
from jax import lax
from jax.sharding import PartitionSpec as P


def solution(mesh):
    def step(x, w_gate, w_up, w_down):
        rows = lax.all_gather(x, "tp", axis=0, tiled=True)
        gate = jnp.dot(rows, w_gate, preferred_element_type=jnp.float32)
        up = jnp.dot(rows, w_up, preferred_element_type=jnp.float32)
        hidden = (jax.nn.silu(gate) * up).astype(jnp.bfloat16)
        term = jnp.dot(hidden, w_down, preferred_element_type=jnp.float32).astype(jnp.bfloat16)
        return lax.psum_scatter(term, "tp", scatter_dimension=0, tiled=True)

    return jax.shard_map(
        step,
        mesh=mesh,
        in_specs=(P(("dp", "tp"), None), P(None, "tp"), P(None, "tp"), P("tp", None)),
        out_specs=P(("dp", "tp"), None),
        check_vma=False,
    )
```

profile of v0, /device:TPU:0, one launch (start us, length us, event | category | flops | bytes accessed | tf_op | source)
XLA Modules:
  0.0 270.2 jit_solution(11089639397008090924)
XLA Ops:
  6.5 0.0 all-gather.2.cloned.1.call-start
  6.5 0.7 all-gather.2.cloned.1.call-update
  7.3 0.0 reduce-scatter.2.cloned.1.call-start
  7.3 60.1 %all-gather.2.cloned.1.call-done = bf16[1024,4096]{1,0:T(8,128)(2,1)} async-done(((bf16[256,4096]{1,0:T(8,128)(2,1)}), bf16[1024,4096]{1,0:T(8,128)(2,1)}) %all-gather.2.cloned.1.call-update) | async-done | bytes 8388624 | tf_op jit(solution)/shard_map/all_gather | solution.py:9
  67.4 0.0 copy-start
  67.4 45.1 %fusion.4 = f32[1024,4096]{1,0:T(8,128)} fusion(bf16[1024,4096]{1,0:T(8,128)(2,1)} %all-gather.2.cloned.1.call-done, bf16[4096,4096]{1,0:T(8,128)(2,1)} %param.5), kind=kOutput, calls=%fused_computation.5 | convolution fusion | flops 34359738368 | bytes 58720256 | tf_op jit(solution)/shard_map/dot_general | solution.py:10
  112.5 0.0 copy-done
  112.6 43.1 %multiply_convert_fusion.clone.6 = bf16[1024,4096]{1,0:T(8,128)(2,1)} fusion(f32[1024,4096]{1,0:T(8,128)} %fusion.4, bf16[1024,4096]{1,0:T(8,128)(2,1)S(1)} %copy-done, bf16[4096,4096]{1,0:T(8,128)(2,1)} %param.6), kind=kOutput, calls=%fused_computation.clone.clone.clone.clone.clone.1 | convolution fusion | flops 34384904192 | bytes 67108864 | tf_op jit(solution)/shard_map/dot_general | solution.py:11
  155.6 42.4 %fusion.2 = bf16[1024,4096]{1,0:T(8,128)(2,1)} fusion(bf16[4096,4096]{1,0:T(8,128)(2,1)} %param.7, bf16[1024,4096]{1,0:T(8,128)(2,1)} %multiply_convert_fusion.clone.6), kind=kOutput, calls=%fused_computation.3 | convolution fusion | flops 34363932672 | bytes 50331648 | tf_op jit(solution)/shard_map/dot_general | solution.py:13
  198.1 0.0 reduce-scatter.2.cloned.1.call-update
  198.1 65.3 %reduce-scatter.2.cloned.1.call-done = bf16[256,4096]{1,0:T(8,128)(2,1)} async-done(((bf16[1024,4096]{1,0:T(8,128)(2,1)}), bf16[256,4096]{1,0:T(8,128)(2,1)}) %reduce-scatter.2.cloned.1.call-update) | async-done | bytes 2097168 | tf_op jit(solution)/shard_map/reduce_scatter | solution.py:14
Async XLA Ops:
  6.5 60.9 %all-gather.2.cloned.1.call-start = ((), (), s32[]{:S(2)}) async-start(), calls=%async_computation.1 | async-start | bytes 10485760 | tf_op jit(solution)/shard_map/all_gather | solution.py:9
  7.3 256.1 %reduce-scatter.2.cloned.1.call-start = ((), (), s32[]{:S(2)}) async-start(), calls=%async_computation.2 | async-start | bytes 10485760 | tf_op jit(solution)/shard_map/reduce_scatter | solution.py:14
  67.4 45.1 %copy-start = (bf16[1024,4096]{1,0:T(8,128)(2,1)S(1)}, bf16[1024,4096]{1,0:T(8,128)(2,1)}, u32[]{:S(2)}) copy-start(bf16[1024,4096]{1,0:T(8,128)(2,1)} %all-gather.2.cloned.1.call-done) | copy-start | bytes 25165828
Sparse Core Ops, SparseCore 0:
  8.9 58.5 all-gather.1
  198.2 65.0 reduce-scatter.1
where the time goes:
time: 270 us
  matrix products  131 us (49%)
  waiting for transfers between devices  126 us (47%)
  between operations  13.4 us (5%)
    reduce_scatter x1, waiting for transfers between devices, step(): return lax.psum_scatter(term, 'tp', scatter_dimension=0, tiled=True)  65.3 us
    all_gather x1, waiting for transfers between devices, step(): rows = lax.all_gather(x, 'tp', axis=0, tiled=True)  60.1 us
    dot_general x1, matrix products, step(): gate = jnp.dot(rows, w_gate, preferred_element_type=jnp.float32)  45.1 us
    dot_general x1, matrix products, step(): up = jnp.dot(rows, w_up, preferred_element_type=jnp.float32)  43.1 us
    dot_general x1, matrix products, step(): jnp.dot(hidden, w_down, preferred_element_type=jnp.float32)  42.4 us
  transfers between devices with their start and end apart: 2, of which 2 were waited for; matrix products, arithmetic and copies ran while one was open for 0% of the time, Pallas kernels for 0%

commit v1 on v0

v1 whole, which is shorter than its diff:
```python
import jax
import jax.numpy as jnp
from jax import lax
from jax.experimental import pallas as pl
from jax.experimental.pallas import tpu as pltpu
from jax.sharding import PartitionSpec as P

MESH = pl.DeviceIdType.MESH
BF16, F32 = jnp.bfloat16, jnp.float32
D = 4096
ROWS = 256
HALF = ROWS // 2
T = 256
GU, DN = D // T, D // (2 * T)
SLOTS = 8
PRE = SLOTS - 1
OWN_ONLY = 3
LATE = 12
N1 = GU
N2 = N1 + LATE
N3 = N2 + DN
N4 = N3 + GU
N5 = N4 + DN
N6 = N5 + DN


def dot(a, b):
    return jnp.dot(a, b, preferred_element_type=F32)


def kernel(
    x_hbm, wg_hbm, wu_hbm, wd_hbm, y_hbm,
    xv, hid, ring, keep, stage, drecv, yrecv, pstage, okeep, ostage,
    wsem, xsem, osem, ag_send, ag_recv, d_send, d_recv, i_send, i_recv, p_send, p_recv,
):
    dp, tp = lax.axis_index("dp"), lax.axis_index("tp")
    chip, core = tp // 2, tp % 2
    mate = (dp, chip * 2 + 1 - core)
    peer = (dp, (1 - chip) * 2 + core)

    def remote(src, dst, send, recv, to):
        return pltpu.make_async_remote_copy(
            src_ref=src, dst_ref=dst, send_sem=send, recv_sem=recv, device_id=to, device_id_type=MESH
        )

    def tile(ref, t, slot, which):
        return pltpu.make_async_copy(
            ref.at[:, pl.ds(pl.multiple_of(t * T, T), T)], ring.at[slot, which], wsem.at[slot, which]
        )

    def fetch_gu(q, t):
        slot = lax.rem(q, SLOTS)
        tile(wg_hbm, t, slot, 0).start()
        tile(wu_hbm, t, slot, 1).start()

    def fetch_dn(q, n):
        slot = lax.rem(q, SLOTS)
        tile(wd_hbm, 2 * n, slot, 0).start()
        tile(wd_hbm, 2 * n + 1, slot, 1).start()

    def fetch(q):
        first = q < N2
        third = jnp.logical_and(q >= N3, q < N4)

        @pl.when(first)
        def _():
            fetch_gu(q, lax.rem(q, GU))

        @pl.when(third)
        def _():
            fetch_gu(q, q - N3)

        @pl.when(jnp.logical_and(q >= N2, q < N3))
        def _():
            fetch_dn(q, q - N2)

        @pl.when(jnp.logical_and(q >= N4, q < N6))
        def _():
            fetch_dn(q, lax.rem(q - N4, DN))

    def arrive(q):
        slot = lax.rem(q, SLOTS)
        tile(wg_hbm, 0, slot, 0).wait()
        tile(wg_hbm, 0, slot, 1).wait()
        fetch(q + PRE)
        return slot

    def gate_up(slot, t, lo, hi, out):
        col = pl.ds(pl.multiple_of(t * T, T), T)
        for r in range(lo, hi, ROWS):
            gate = dot(xv[r : r + ROWS, :], ring[slot, 0])
            up = dot(xv[r : r + ROWS, :], ring[slot, 1])
            hid[out + r - lo : out + r - lo + ROWS, col] = (jax.nn.silu(gate) * up).astype(BF16)

    own = pltpu.make_async_copy(x_hbm, xv.at[pl.ds(0, ROWS)], xsem)
    own.start()
    fetch_gu(0, 0)
    fetch_gu(1, 1)
    barrier = pltpu.get_barrier_semaphore()
    for to in (mate, peer):
        pl.semaphore_signal(barrier, inc=1, device_id=to, device_id_type=MESH)
    pl.semaphore_wait(barrier, 2)
    near = remote(x_hbm, xv.at[pl.ds(ROWS, ROWS)], ag_send.at[0], ag_recv.at[0], mate)
    near.start()

    def far(h):
        return remote(
            x_hbm.at[pl.ds(h * HALF, HALF)],
            xv.at[pl.ds((2 + h) * ROWS, HALF)],
            ag_send.at[1 + h], ag_recv.at[1 + h], peer,
        )

    def forward(h):
        return remote(
            xv.at[pl.ds((2 + h) * ROWS, HALF)],
            xv.at[pl.ds((2 + h) * ROWS + HALF, HALF)],
            ag_send.at[3 + h], ag_recv.at[3 + h], mate,
        )

    far(0).start()
    far(1).start()
    for q in range(2, PRE):
        fetch_gu(q, q)
    own.wait()

    def pass_own(t, _):
        slot = arrive(t)
        gate_up(slot, t, 0, ROWS, 0)
        return 0

    lax.fori_loop(0, OWN_ONLY, pass_own, 0)
    near.wait_recv()

    def pass_near(t, _):
        @pl.when(t == LATE - 1)
        def _():
            far(0).wait_recv()
            forward(0).start()

        slot = arrive(t)
        gate_up(slot, t, 0, 2 * ROWS, 0)
        return 0

    lax.fori_loop(OWN_ONLY, LATE, pass_near, 0)
    near.wait_send()
    forward(0).wait()

    def pass_three(t, _):
        slot = arrive(t)
        gate_up(slot, t, 0, 3 * ROWS, 0)
        return 0

    lax.fori_loop(LATE, GU, pass_three, 0)

    def pass_mixed(t, _):
        slot = arrive(t + N1)
        gate_up(slot, t, ROWS, 3 * ROWS, ROWS)
        return 0

    lax.fori_loop(0, OWN_ONLY, pass_mixed, 0)

    def pass_far(t, _):
        slot = arrive(t + N1)
        gate_up(slot, t, 2 * ROWS, 3 * ROWS, 2 * ROWS)
        return 0

    lax.fori_loop(OWN_ONLY, LATE, pass_far, 0)
    far(1).wait_recv()
    forward(1).start()

    def to_mate(h, n):
        k = h * DN + n
        return remote(stage.at[lax.rem(n, 4)], drecv.at[k], d_send.at[k], d_recv.at[k], mate)

    def to_peer(h, n):
        k = h * DN + n
        return remote(drecv.at[k], yrecv.at[k], i_send.at[k], i_recv.at[k], peer)

    def tick(h, n):
        @pl.when(jnp.logical_and(n >= 1, n <= DN))
        def _():
            to_mate(h, n - 1).start()

        @pl.when(jnp.logical_and(n >= 3, n <= DN + 2))
        def _():
            to_peer(h, n - 3).start()

        @pl.when(jnp.logical_and(n >= 2, n <= DN + 1))
        def _():
            m = n - 2
            to_mate(h, m).wait()
            k = h * DN + m
            drecv[k] = (keep[lax.rem(m, 4)] + drecv[k].astype(F32)).astype(BF16)

    def down_far(h, base):
        def body(n, _):
            tick(h, n)
            slot = arrive(base + n)
            for w in range(2):
                term = dot(hid[2 * ROWS :, :], ring[slot, w])
                keep[lax.rem(n, 4), :, w * T : (w + 1) * T] = term[:HALF]
                stage[lax.rem(n, 4), :, w * T : (w + 1) * T] = term[HALF:].astype(BF16)
            return 0

        lax.fori_loop(0, DN, body, 0)

    down_far(0, N2)
    forward(1).wait()
    far(0).wait_send()
    far(1).wait_send()

    def pass_last(t, _):
        tick(0, t + DN)
        slot = arrive(t + N3)
        gate_up(slot, t, 3 * ROWS, 4 * ROWS, 2 * ROWS)
        return 0

    lax.fori_loop(0, GU, pass_last, 0)
    down_far(1, N4)

    def columns(n):
        return pl.ds(pl.multiple_of(n * 2 * T, 2 * T), 2 * T)

    def rows_to_mate(n):
        return remote(
            pstage.at[lax.rem(n, 4)],
            xv.at[pl.ds(2 * ROWS, ROWS), columns(n)],
            p_send.at[n], p_recv.at[n], mate,
        )

    def write(n):
        s = lax.rem(n, 2)
        return pltpu.make_async_copy(ostage.at[s], y_hbm.at[:, columns(n)], osem.at[s])

    def finish(n):
        rows_to_mate(n).wait()
        to_peer(0, n).wait_recv()
        to_peer(1, n).wait_recv()
        near_term = xv[2 * ROWS : 3 * ROWS, columns(n)].astype(F32)
        s = lax.rem(n, 4)
        for h in range(2):
            r = slice(h * HALF, (h + 1) * HALF)
            total = okeep[s, r] + near_term[r] + yrecv[h * DN + n].astype(F32)
            ostage[lax.rem(n, 2), r] = total.astype(BF16)
        write(n).start()

    def down_near(n, _):
        @pl.when(n >= 1)
        def _():
            rows_to_mate(n - 1).start()

        tick(1, n + DN)

        @pl.when(n >= 4)
        def _():
            write(n - 4).wait()

        @pl.when(n >= 2)
        def _():
            finish(n - 2)

        slot = arrive(N5 + n)
        s = lax.rem(n, 4)
        for w in range(2):
            c = slice(w * T, (w + 1) * T)
            pstage[s, :, c] = dot(hid[ROWS : 2 * ROWS, :], ring[slot, w]).astype(BF16)
        for w in range(2):
            c = slice(w * T, (w + 1) * T)
            okeep[s, :, c] = dot(hid[:ROWS, :], ring[slot, w])
        return 0

    lax.fori_loop(0, DN, down_near, 0)
    rows_to_mate(DN - 1).start()
    for n in (DN - 2, DN - 1):
        write(n - 2).wait()
        finish(n)
    for n in (DN - 2, DN - 1):
        write(n).wait()

    for h in range(2):

        def drain(n, _):
            to_peer(h, n).wait_send()
            return 0

        lax.fori_loop(0, DN, drain, 0)


def solution(mesh):
    def step(x, w_gate, w_up, w_down):
        dma = pltpu.SemaphoreType.DMA
        return pl.pallas_call(
            kernel,
            out_shape=jax.ShapeDtypeStruct((ROWS, D), BF16),
            in_specs=[pl.BlockSpec(memory_space=pltpu.HBM)] * 4,
            out_specs=pl.BlockSpec(memory_space=pltpu.HBM),
            scratch_shapes=[
                pltpu.VMEM((4 * ROWS, D), BF16),
                pltpu.VMEM((3 * ROWS, D), BF16),
                pltpu.VMEM((SLOTS, 2, D, T), BF16),
                pltpu.VMEM((4, HALF, 2 * T), F32),
                pltpu.VMEM((4, HALF, 2 * T), BF16),
                pltpu.VMEM((2 * DN, HALF, 2 * T), BF16),
                pltpu.VMEM((2 * DN, HALF, 2 * T), BF16),
                pltpu.VMEM((4, ROWS, 2 * T), BF16),
                pltpu.VMEM((4, ROWS, 2 * T), F32),
                pltpu.VMEM((2, ROWS, 2 * T), BF16),
                dma((SLOTS, 2)),
                dma,
                dma((2,)),
                dma((5,)),
                dma((5,)),
                dma((2 * DN,)),
                dma((2 * DN,)),
                dma((2 * DN,)),
                dma((2 * DN,)),
                dma((DN,)),
                dma((DN,)),
            ],
            compiler_params=pltpu.CompilerParams(
                collective_id=0, has_side_effects=True, vmem_limit_bytes=67043328
            ),
            name="mlp",
        )(x, w_gate, w_up, w_down)

    return jax.shard_map(
        step,
        mesh=mesh,
        in_specs=(P(("dp", "tp"), None), P(None, "tp"), P(None, "tp"), P("tp", None)),
        out_specs=P(("dp", "tp"), None),
        check_vma=False,
    )
```

time: 270 us -> 130 us (0.48)
  matrix products: 131 us -> 0 us
  Pallas kernels: 0 us -> 127 us
  waiting for transfers between devices: 126 us -> 0 us
  between operations: 13.4 us -> 0.01 us
  local copies, waits for them, and re-layouts: 0.01 us -> 3.13 us
    dot_general x3 -> x0, matrix products: 131 us -> none  [the longest x1 45.1 us: step(): gate = jnp.dot(rows, w_gate, preferred_element_type=jnp.float32)]
    pallas_call x0 -> x1, Pallas kernels: none -> 127 us  [step(): pl.pallas_call(kernel, out_shape=jax.ShapeDtypeStruct((ROWS, D), BF16), i...]
    reduce_scatter x1 -> x0, waiting for transfers between devices: 65.3 us -> none  [step(): return lax.psum_scatter(term, 'tp', scatter_dimension=0, tiled=True)]
    all_gather x1 -> x0, waiting for transfers between devices: 60.1 us -> none  [step(): rows = lax.all_gather(x, 'tp', axis=0, tiled=True)]
    unnamed x2 -> x1, local copies, waits for them, and re-layouts: 0.01 us -> 3.13 us
  transfers between devices with their start and end apart: 2 -> 0, of which waited for: 2 -> 0; matrix products, arithmetic and copies ran while one was open for 0% -> 0% of each run, Pallas kernels for 0% -> 0%
where the time goes in v1:
time: 130 us
  Pallas kernels  127 us (98%)
  local copies, waits for them, and re-layouts  3.13 us (2%)
    pallas_call x1, Pallas kernels, step(): pl.pallas_call(kernel, out_shape=jax.ShapeDtypeStruct((ROWS, D), BF16), i...  127 us
    unnamed x1, local copies, waits for them, and re-layouts  3.13 us

profile of v1, /device:TPU:0, one launch (start us, length us, event | category | flops | bytes accessed | tf_op | source)
XLA Modules:
  0.0 129.7 jit_solution(10201121295778586818)
XLA Ops:
  0.0 126.5 %mlp.1 = bf16[256,4096]{1,0:T(8,128)(2,1)} custom-call(bf16[256,4096]{1,0:T(8,128)(2,1)} %x_hbm.1, bf16[4096,4096]{1,0:T(8,128)(2,1)} %wg_hbm.1, bf16[4096,4096]{1,0:T(8,128)(2,1)} %wu_hbm.1, bf16[4096,4096]{1,0:T(8,128)(2,1)} %wd_hbm.1), custom_call_target="tpu_custom_call" | custom-call | tf_op jit(solution)/shard_map/mlp/pallas_call | solution.py:292
  126.5 3.1 %copy.6 = bf16[256,4096]{1,0:T(8,128)(2,1)} copy(bf16[256,4096]{1,0:T(8,128)(2,1)} %mlp.1) | data formatting | bytes 4194304

commit v2 on v0

v2 whole, which is shorter than its diff:
```python
import jax
import jax.numpy as jnp
from jax import lax
from jax.experimental import pallas as pl
from jax.experimental.pallas import tpu as pltpu
from jax.sharding import PartitionSpec as P

MESH = pl.DeviceIdType.MESH
BF16, F32 = jnp.bfloat16, jnp.float32
D = 4096
ROWS = 256
HALF = ROWS // 2
T = 256
W = 2 * T
GU, DN = D // T, D // W
SLOTS = 8
LEFT = 2
LATE = GU - 2
PASS = GU + DN
REST = LATE + 2 * PASS
LAST = REST + GU - LATE + LEFT
O, M, R = 0, ROWS, 2 * ROWS


def dot(a, b):
    return jnp.dot(a, b, preferred_element_type=F32)


def kernel(
    x_hbm, wg_hbm, wu_hbm, wd_hbm, y_hbm,
    xv, hid, ring, keep, stage, drecv, yrecv, ostage,
    wsem, xsem, osem, ag_send, ag_recv, d_send, d_recv, i_send, i_recv, p_send, p_recv,
):
    dp, tp = lax.axis_index("dp"), lax.axis_index("tp")
    chip, core = tp // 2, tp % 2
    mate = (dp, chip * 2 + 1 - core)
    peer = (dp, (1 - chip) * 2 + core)

    def remote(src, dst, send, recv, to):
        return pltpu.make_async_remote_copy(
            src_ref=src, dst_ref=dst, send_sem=send, recv_sem=recv, device_id=to, device_id_type=MESH
        )

    def tile(ref, t, slot, which):
        return pltpu.make_async_copy(
            ref.at[:, pl.ds(pl.multiple_of(t * T, T), T)], ring.at[slot, which], wsem.at[slot, which]
        )

    def fetch_gu(q, t):
        slot = lax.rem(q, SLOTS)
        tile(wg_hbm, t, slot, 0).start()
        tile(wu_hbm, t, slot, 1).start()

    def fetch_dn(q, n):
        slot = lax.rem(q, SLOTS)
        tile(wd_hbm, 2 * n, slot, 0).start()
        tile(wd_hbm, 2 * n + 1, slot, 1).start()

    def arrive(q):
        slot = lax.rem(q, SLOTS)
        tile(wg_hbm, 0, slot, 0).wait()
        tile(wg_hbm, 0, slot, 1).wait()

    def gate_up(q, t, row, out):
        slot = lax.rem(q, SLOTS)
        x = xv[pl.ds(row, ROWS), :]
        gate = dot(x, ring[slot, 0])
        up = dot(x, ring[slot, 1])
        hid[pl.ds(out, ROWS), pl.ds(pl.multiple_of(t * T, T), T)] = (jax.nn.silu(gate) * up).astype(BF16)

    own = pltpu.make_async_copy(x_hbm, xv.at[pl.ds(O, ROWS)], xsem)
    own.start()
    fetch_gu(0, 0)
    fetch_gu(1, 1)
    barrier = pltpu.get_barrier_semaphore()
    for to in (mate, peer):
        pl.semaphore_signal(barrier, inc=1, device_id=to, device_id_type=MESH)
    pl.semaphore_wait(barrier, 2)
    near = remote(x_hbm, xv.at[pl.ds(M, ROWS)], ag_send.at[0], ag_recv.at[0], mate)
    near.start()

    def far(h):
        return remote(
            x_hbm.at[pl.ds(h * HALF, HALF)], xv.at[pl.ds(R + h * ROWS, HALF)], ag_send.at[1 + h], ag_recv.at[1 + h], peer
        )

    def forward(h):
        return remote(
            xv.at[pl.ds(R + h * ROWS, HALF)],
            xv.at[pl.ds(R + h * ROWS + HALF, HALF)],
            ag_send.at[3 + h], ag_recv.at[3 + h], mate,
        )

    far(0).start()
    far(1).start()
    for q in range(2, SLOTS):
        fetch_gu(q, q)
    own.wait()

    def pass_own(q, _):
        arrive(q)
        gate_up(q, q, O, O)
        fetch_gu(q + SLOTS, q + SLOTS)
        return 0

    lax.fori_loop(0, LEFT, pass_own, 0)
    near.wait()

    def pass_near(j, _):
        q = LEFT + 2 * j

        @pl.when(j == (LATE - LEFT) // 2 - 1)
        def _():
            far(0).wait_recv()
            forward(0).start()

        for u in range(2):
            arrive(q + u)
        for u in range(2):
            gate_up(q + u, q + u, O, O)
            gate_up(q + u, q + u, M, M)
        for u in range(2):
            fetch_gu(q + u + SLOTS, lax.rem(q + u + SLOTS, LATE))
        return 0

    lax.fori_loop(0, (LATE - LEFT) // 2, pass_near, 0)
    forward(0).wait()

    def to_mate(h, n):
        k = h * DN + n
        return remote(stage.at[lax.rem(n, 4), pl.ds(0, HALF)], drecv.at[k], d_send.at[k], d_recv.at[k], mate)

    def to_peer(h, n):
        k = h * DN + n
        return remote(drecv.at[k], yrecv.at[k], i_send.at[k], i_recv.at[k], peer)

    def combine(h, d):
        for u in range(2):
            n = 2 * d + u
            to_mate(h, n).wait()
            k = h * DN + n
            drecv[k] = (keep[lax.rem(n, 6), :HALF] + drecv[k].astype(F32)).astype(BF16)

    def send_terms(h, d):
        for u in range(2):
            to_mate(h, 2 * d + u).start()

    def send_sums(h, d):
        for u in range(2):
            to_peer(h, 2 * d + u).start()

    def tail(h, j):
        @pl.when(j == 0)
        def _():
            send_terms(h, 3)
            combine(h, 2)
            send_sums(h, 2)

        @pl.when(j == 1)
        def _():
            combine(h, 3)
            send_sums(h, 3)

    def half(h, _):
        base = LATE + PASS * h
        row = pl.multiple_of(R + h * ROWS, ROWS)

        def gate_up_far(j, _):
            q = base + 2 * j

            @pl.when(jnp.logical_and(h == 1, j < 2))
            def _():
                tail(0, j)

            for u in range(2):
                arrive(q + u)
            for u in range(2):
                gate_up(q + u, 2 * j + u, row, R)

            @pl.when(j < 4)
            def _():
                for u in range(2):
                    fetch_gu(q + u + SLOTS, 2 * j + u + SLOTS)

            @pl.when(j >= 4)
            def _():
                for u in range(2):
                    fetch_dn(q + u + SLOTS, 2 * j + u + SLOTS - GU)

            return 0

        lax.fori_loop(0, GU // 2, gate_up_far, 0)

        @pl.when(h == 0)
        def _():
            far(1).wait_recv()
            forward(1).start()

        def down_far(d, _):
            q = base + GU + 2 * d

            @pl.when(d >= 1)
            def _():
                send_terms(h, d - 1)

            @pl.when(d >= 2)
            def _():
                combine(h, d - 2)
                send_sums(h, d - 2)

            for u in range(2):
                arrive(q + u)
            for u in range(2):
                slot, n = lax.rem(q + u, SLOTS), 2 * d + u
                for w in range(2):
                    c = slice(w * T, (w + 1) * T)
                    term = dot(hid[R:, :], ring[slot, w])
                    keep[lax.rem(n, 6), :HALF, c] = term[:HALF]
                    stage[lax.rem(n, 4), :HALF, c] = term[HALF:].astype(BF16)

            @pl.when(h == 0)
            def _():
                for u in range(2):
                    fetch_gu(q + u + SLOTS, 2 * d + u)

            @pl.when(jnp.logical_and(h == 1, d < 2))
            def _():
                for u in range(2):
                    fetch_gu(q + u + SLOTS, lax.rem(LATE + 2 * d + u, GU))

            @pl.when(jnp.logical_and(h == 1, d >= 2))
            def _():
                for u in range(2):
                    fetch_dn(q + u + SLOTS, 2 * d + u - 4)

            return 0

        lax.fori_loop(0, DN // 2, down_far, 0)

        @pl.when(h == 0)
        def _():
            forward(1).wait()

        return 0

    lax.fori_loop(0, 2, half, 0)
    far(0).wait_send()
    far(1).wait_send()

    for j, (steps, rows) in enumerate(((range(LATE, GU), (O, M)), (range(LEFT), (M,)))):
        tail(1, j)
        q = REST + 2 * j
        for u in range(2):
            arrive(q + u)
        for u, t in enumerate(steps):
            for r in rows:
                gate_up(q + u, t, r, r)
        for u in range(2):
            fetch_dn(q + u + SLOTS, q + u + SLOTS - LAST)

    def columns(n):
        return pl.ds(pl.multiple_of(n * W, W), W)

    def rows_to_mate(n):
        return remote(
            stage.at[lax.rem(n, 4)], xv.at[pl.ds(R, ROWS), columns(n)], p_send.at[n], p_recv.at[n], mate
        )

    def send_rows(j):
        for u in range(2):
            rows_to_mate(2 * j + u).start()

    def take(j):
        for u in range(2):
            n = 2 * j + u
            rows_to_mate(n).wait()
            to_peer(0, n).wait_recv()
            to_peer(1, n).wait_recv()

    def total(j):
        for n in (2 * j, 2 * j + 1):
            for h in range(2):
                r = slice(h * HALF, (h + 1) * HALF)
                mates = xv[R + h * HALF : R + (h + 1) * HALF, n * W : (n + 1) * W].astype(F32)
                y = keep[n % 6, r] + mates + yrecv[h * DN + n].astype(F32)
                ostage[n % 4, r] = y.astype(BF16)

    def write(n):
        s = n % 4
        return pltpu.make_async_copy(ostage.at[s], y_hbm.at[:, pl.ds(n * W, W)], osem.at[s])

    def write_out(j):
        for u in range(2):
            write(2 * j + u).start()

    def written(j):
        for u in range(2):
            write(2 * j + u).wait()

    def mates_rows(j):
        for u in range(2):
            n = 2 * j + u
            slot = lax.rem(LAST + n, SLOTS)
            for w in range(2):
                stage[lax.rem(n, 4), :, w * T : (w + 1) * T] = dot(hid[M:R, :], ring[slot, w]).astype(BF16)

    def own_rows(j):
        for u in range(2):
            n = 2 * j + u
            slot = lax.rem(LAST + n, SLOTS)
            for w in range(2):
                keep[lax.rem(n, 6), :, w * T : (w + 1) * T] = dot(hid[O:M, :], ring[slot, w])

    def arrived(j):
        for u in range(2):
            arrive(LAST + 2 * j + u)

    def down_own(j, _):
        pl.when(j == 1)(lambda: send_rows(0))
        arrived(j)
        mates_rows(j)
        own_rows(j)
        return 0

    lax.fori_loop(0, 2, down_own, 0)
    send_rows(1)
    take(0)
    arrived(2)
    total(0)
    mates_rows(2)
    own_rows(2)

    send_rows(2)
    write_out(0)
    take(1)
    arrived(3)
    total(1)
    mates_rows(3)

    send_rows(3)
    write_out(1)
    take(2)
    written(0)
    total(2)
    own_rows(3)

    write_out(2)
    take(3)
    written(1)
    total(3)
    write_out(3)

    for h in range(2):

        def drain(n, _):
            to_peer(h, n).wait_send()
            return 0

        lax.fori_loop(0, DN, drain, 0)
    written(2)
    written(3)


def solution(mesh):
    def step(x, w_gate, w_up, w_down):
        dma = pltpu.SemaphoreType.DMA
        return pl.pallas_call(
            kernel,
            out_shape=jax.ShapeDtypeStruct((ROWS, D), BF16),
            in_specs=[pl.BlockSpec(memory_space=pltpu.HBM)] * 4,
            out_specs=pl.BlockSpec(memory_space=pltpu.HBM),
            scratch_shapes=[
                pltpu.VMEM((4 * ROWS, D), BF16),
                pltpu.VMEM((3 * ROWS, D), BF16),
                pltpu.VMEM((SLOTS, 2, D, T), BF16),
                pltpu.VMEM((6, ROWS, W), F32),
                pltpu.VMEM((4, ROWS, W), BF16),
                pltpu.VMEM((2 * DN, HALF, W), BF16),
                pltpu.VMEM((2 * DN, HALF, W), BF16),
                pltpu.VMEM((4, ROWS, W), BF16),
                dma((SLOTS, 2)),
                dma,
                dma((4,)),
                dma((5,)),
                dma((5,)),
                dma((2 * DN,)),
                dma((2 * DN,)),
                dma((2 * DN,)),
                dma((2 * DN,)),
                dma((DN,)),
                dma((DN,)),
            ],
            compiler_params=pltpu.CompilerParams(
                collective_id=0, has_side_effects=True, vmem_limit_bytes=67043328
            ),
            name="mlp",
        )(x, w_gate, w_up, w_down)

    return jax.shard_map(
        step,
        mesh=mesh,
        in_specs=(P(("dp", "tp"), None), P(None, "tp"), P(None, "tp"), P("tp", None)),
        out_specs=P(("dp", "tp"), None),
        check_vma=False,
    )
```

time: 270 us -> 122 us (0.45)
  matrix products: 131 us -> 0 us
  waiting for transfers between devices: 126 us -> 0 us
  Pallas kernels: 0 us -> 119 us
  between operations: 13.4 us -> 0.01 us
  local copies, waits for them, and re-layouts: 0.01 us -> 3.13 us
    dot_general x3 -> x0, matrix products: 131 us -> none  [the longest x1 45.1 us: step(): gate = jnp.dot(rows, w_gate, preferred_element_type=jnp.float32)]
    pallas_call x0 -> x1, Pallas kernels: none -> 119 us  [step(): pl.pallas_call(kernel, out_shape=jax.ShapeDtypeStruct((ROWS, D), BF16), i...]
    reduce_scatter x1 -> x0, waiting for transfers between devices: 65.3 us -> none  [step(): return lax.psum_scatter(term, 'tp', scatter_dimension=0, tiled=True)]
    all_gather x1 -> x0, waiting for transfers between devices: 60.1 us -> none  [step(): rows = lax.all_gather(x, 'tp', axis=0, tiled=True)]
    unnamed x2 -> x1, local copies, waits for them, and re-layouts: 0.01 us -> 3.13 us
  transfers between devices with their start and end apart: 2 -> 0, of which waited for: 2 -> 0; matrix products, arithmetic and copies ran while one was open for 0% -> 0% of each run, Pallas kernels for 0% -> 0%
where the time goes in v2:
time: 122 us
  Pallas kernels  119 us (98%)
  local copies, waits for them, and re-layouts  3.13 us (3%)
    pallas_call x1, Pallas kernels, step(): pl.pallas_call(kernel, out_shape=jax.ShapeDtypeStruct((ROWS, D), BF16), i...  119 us
    unnamed x1, local copies, waits for them, and re-layouts  3.13 us

profile of v2, /device:TPU:0, one launch (start us, length us, event | category | flops | bytes accessed | tf_op | source)
XLA Modules:
  0.0 122.3 jit_solution(17473494055667043430)
XLA Ops:
  0.0 119.1 %mlp.1 = bf16[256,4096]{1,0:T(8,128)(2,1)} custom-call(bf16[256,4096]{1,0:T(8,128)(2,1)} %x_hbm.1, bf16[4096,4096]{1,0:T(8,128)(2,1)} %wg_hbm.1, bf16[4096,4096]{1,0:T(8,128)(2,1)} %wu_hbm.1, bf16[4096,4096]{1,0:T(8,128)(2,1)} %wd_hbm.1), custom_call_target="tpu_custom_call" | custom-call | tf_op jit(solution)/shard_map/mlp/pallas_call | solution.py:367
  119.1 3.1 %copy.6 = bf16[256,4096]{1,0:T(8,128)(2,1)} copy(bf16[256,4096]{1,0:T(8,128)(2,1)} %mlp.1) | data formatting | bytes 4194304

commit v3 on v0

v3 whole, which is shorter than its diff:
```python
import jax
import jax.numpy as jnp
from jax import lax
from jax.experimental import pallas as pl
from jax.experimental.pallas import tpu as pltpu
from jax.sharding import PartitionSpec as P

MESH = pl.DeviceIdType.MESH
BF16, F32 = jnp.bfloat16, jnp.float32
D = 4096
ROWS = 256
HALF = ROWS // 2
T = 256
W = 2 * T
GU, DN = D // T, D // W
SLOTS = 10
LEFT = 2
LATE = GU - 2
PASS = GU + DN
REST = LATE + 2 * PASS
LAST = REST + GU - LATE + LEFT
O, M, R = 0, ROWS, 2 * ROWS


def dot(a, b):
    return jnp.dot(a, b, preferred_element_type=F32)


def kernel(
    x_hbm, wg_hbm, wu_hbm, wd_hbm, y_hbm,
    xv, hid, ring, keep, stage, drecv, yrecv,
    wsem, xsem, osem, ag_send, ag_recv, d_send, d_recv, i_send, i_recv, p_send, p_recv, free,
):
    dp, tp = lax.axis_index("dp"), lax.axis_index("tp")
    chip, core = tp // 2, tp % 2
    mate = (dp, chip * 2 + 1 - core)
    peer = (dp, (1 - chip) * 2 + core)

    def remote(src, dst, send, recv, to):
        return pltpu.make_async_remote_copy(
            src_ref=src, dst_ref=dst, send_sem=send, recv_sem=recv, device_id=to, device_id_type=MESH
        )

    def tile(ref, t, slot, which):
        return pltpu.make_async_copy(
            ref.at[:, pl.ds(pl.multiple_of(t * T, T), T)], ring.at[slot, which], wsem.at[slot, which]
        )

    def fetch_gu(q, t):
        slot = lax.rem(q, SLOTS)
        tile(wg_hbm, t, slot, 0).start()
        tile(wu_hbm, t, slot, 1).start()

    def fetch_dn(q, n):
        slot = lax.rem(q, SLOTS)
        tile(wd_hbm, 2 * n, slot, 0).start()
        tile(wd_hbm, 2 * n + 1, slot, 1).start()

    def arrive(q):
        slot = lax.rem(q, SLOTS)
        tile(wg_hbm, 0, slot, 0).wait()
        tile(wg_hbm, 0, slot, 1).wait()

    def gate_up(q, t, row, out):
        slot = lax.rem(q, SLOTS)
        x = xv[pl.ds(row, ROWS), :]
        gate = dot(x, ring[slot, 0])
        up = dot(x, ring[slot, 1])
        hid[pl.ds(out, ROWS), pl.ds(pl.multiple_of(t * T, T), T)] = (jax.nn.silu(gate) * up).astype(BF16)

    own = pltpu.make_async_copy(x_hbm, xv.at[pl.ds(O, ROWS)], xsem)
    own.start()
    fetch_gu(0, 0)
    fetch_gu(1, 1)
    barrier = pltpu.get_barrier_semaphore()
    for to in (mate, peer):
        pl.semaphore_signal(barrier, inc=1, device_id=to, device_id_type=MESH)
    pl.semaphore_wait(barrier, 2)
    near = remote(x_hbm, xv.at[pl.ds(M, ROWS)], ag_send.at[0], ag_recv.at[0], mate)
    near.start()

    def far(h):
        return remote(
            x_hbm.at[pl.ds(h * HALF, HALF)], xv.at[pl.ds(R + h * ROWS, HALF)], ag_send.at[1 + h], ag_recv.at[1 + h], peer
        )

    def forward(h):
        return remote(
            xv.at[pl.ds(R + h * ROWS, HALF)],
            xv.at[pl.ds(R + h * ROWS + HALF, HALF)],
            ag_send.at[3 + h], ag_recv.at[3 + h], mate,
        )

    far(0).start()
    far(1).start()
    for q in range(2, SLOTS):
        fetch_gu(q, q)
    own.wait()

    def pass_own(q, _):
        arrive(q)
        gate_up(q, q, O, O)
        fetch_gu(q + SLOTS, q + SLOTS)
        return 0

    lax.fori_loop(0, LEFT, pass_own, 0)
    near.wait()

    def pass_near(q, u):
        for i in range(u):
            arrive(q + i)
        for i in range(u):
            gate_up(q + i, q + i, O, O)
            gate_up(q + i, q + i, M, M)
        for i in range(u):
            fetch_gu(q + i + SLOTS, lax.rem(q + i + SLOTS, LATE))

    def pass_single(q, _):
        pass_near(q, 1)
        return 0

    lax.fori_loop(LEFT, LEFT + 2, pass_single, 0)

    def pass_double(j, _):
        @pl.when(j == LATE // 2 - 1)
        def _():
            far(0).wait_recv()
            forward(0).start()

        pass_near(2 * j, 2)
        return 0

    lax.fori_loop(LEFT // 2 + 1, LATE // 2, pass_double, 0)
    forward(0).wait()

    def place(n, part):
        return pl.ds(R + ROWS + part * HALF, HALF), pl.ds(n * W, W)

    def terms(h, n):
        return xv.at[place(n, 0)] if h else drecv.at[n]

    def sums(h, n):
        return xv.at[place(n, 1)] if h else yrecv.at[n]

    def to_mate(h, d, i):
        n = 4 * d + i
        k = h * DN + n
        src = stage.at[2 * d + i // 2, pl.ds(i % 2 * HALF, HALF)]
        return remote(src, terms(h, n), d_send.at[k], d_recv.at[k], mate)

    def to_peer(h, n):
        k = h * DN + n
        return remote(terms(h, n), sums(h, n), i_send.at[k], i_recv.at[k], peer)

    def send_terms(h, d):
        for i in range(4):
            to_mate(h, d, i).start()

    def combine(h, d):
        for i in range(4):
            to_mate(h, d, i).wait()
        for i in range(4):
            at = terms(h, 4 * d + i)
            mine = keep[2 * d + i // 2, i % 2 * HALF : (i % 2 + 1) * HALF]
            at[...] = (mine + at[...].astype(F32)).astype(BF16)

    def send_sums(h, d):
        for i in range(4):
            to_peer(h, 4 * d + i).start()

    def half(h, _):
        base = LATE + PASS * h
        row = pl.multiple_of(R + h * ROWS, ROWS)

        def gate_up_far(j, _):
            q = base + 4 * j

            @pl.when(jnp.logical_and(h == 1, j == 0))
            def _():
                combine(0, 0)
                send_terms(0, 1)
                send_sums(0, 0)

            @pl.when(jnp.logical_and(h == 1, j == 1))
            def _():
                combine(0, 1)

            for i in range(4):
                arrive(q + i)

            @pl.when(jnp.logical_and(h == 1, j == 1))
            def _():
                send_sums(0, 1)

            for i in range(4):
                gate_up(q + i, 4 * j + i, row, R)

            @pl.when(j < 2)
            def _():
                for i in range(2):
                    fetch_gu(q + i + SLOTS, 4 * j + i + SLOTS)

            @pl.when(j >= 2)
            def _():
                for i in range(2):
                    fetch_dn(q + i + SLOTS, 4 * j + i + SLOTS - GU)

            @pl.when(j < 1)
            def _():
                for i in range(2, 4):
                    fetch_gu(q + i + SLOTS, 4 * j + i + SLOTS)

            @pl.when(jnp.logical_and(j >= 1, j < 3))
            def _():
                for i in range(2, 4):
                    fetch_dn(q + i + SLOTS, 4 * j + i + SLOTS - GU)

            @pl.when(j == 3)
            def _():
                for i in range(2):
                    fetch_gu(q + i + 2 + SLOTS, LATE * h + i)

            return 0

        lax.fori_loop(0, GU // 4, gate_up_far, 0)

        @pl.when(h == 0)
        def _():
            far(1).wait_recv()
            forward(1).start()

        @pl.when(h == 1)
        def _():
            for i, to in enumerate((mate, peer)):
                pl.semaphore_signal(free.at[i], inc=1, device_id=to, device_id_type=MESH)

        def down_far(d, _):
            q = base + GU + 4 * d

            @pl.when(jnp.logical_and(d == 1, h == 0))
            def _():
                send_terms(0, 0)

            @pl.when(jnp.logical_and(d == 1, h == 1))
            def _():
                pl.semaphore_wait(free.at[0], 1)
                send_terms(1, 0)

            for i in range(4):
                arrive(q + i)
            for i in range(4):
                slot = lax.rem(q + i, SLOTS)
                r = slice(i % 2 * HALF, (i % 2 + 1) * HALF)
                for w in range(2):
                    c = slice(w * T, (w + 1) * T)
                    term = dot(hid[R:, :], ring[slot, w])
                    keep[2 * d + i // 2, r, c] = term[:HALF]
                    stage[2 * d + i // 2, r, c] = term[HALF:].astype(BF16)

            @pl.when(h == 0)
            def _():
                for i in range(4):
                    fetch_gu(q + i + SLOTS, 4 * d + i + 2)

            @pl.when(jnp.logical_and(h == 1, d == 0))
            def _():
                for i in range(2):
                    fetch_gu(q + i + SLOTS, i)
                for i in range(2):
                    fetch_dn(q + i + 2 + SLOTS, i)

            @pl.when(jnp.logical_and(h == 1, d == 1))
            def _():
                for i in range(4):
                    fetch_dn(q + i + SLOTS, i + 2)

            return 0

        lax.fori_loop(0, DN // 4, down_far, 0)

        @pl.when(h == 0)
        def _():
            forward(1).wait()

        return 0

    lax.fori_loop(0, 2, half, 0)
    far(0).wait_send()
    far(1).wait_send()

    combine(1, 0)
    send_terms(1, 1)
    pl.semaphore_wait(free.at[1], 1)
    send_sums(1, 0)
    steps = (*range(LATE, GU), *range(LEFT))
    for i in range(4):
        arrive(REST + i)
    for i, t in enumerate(steps):
        for r in (O, M) if t >= LATE else (M,):
            gate_up(REST + i, t, r, r)
    for i in range(2):
        fetch_dn(REST + i + SLOTS, DN - 2 + i)
    combine(1, 1)

    def rows_to_mate(n):
        return remote(stage.at[n], xv.at[pl.ds(R, ROWS), pl.ds(n * W, W)], p_send.at[n], p_recv.at[n], mate)

    def write(n):
        return pltpu.make_async_copy(stage.at[n], y_hbm.at[:, pl.ds(n * W, W)], osem.at[n])

    def each(what, *steps):
        for n in steps:
            what(n)

    def send_rows(n):
        rows_to_mate(n).start()

    def take(n):
        rows_to_mate(n).wait()
        to_peer(0, n).wait_recv()
        to_peer(1, n).wait_recv()

    def total(n):
        for h in range(2):
            r = slice(h * HALF, (h + 1) * HALF)
            mates = xv[R + h * HALF : R + (h + 1) * HALF, n * W : (n + 1) * W].astype(F32)
            y = keep[n % 6, r] + mates + sums(h, n)[...].astype(F32)
            stage[n, r] = y.astype(BF16)

    def write_out(n):
        write(n).start()

    def mates_rows(n):
        for w in range(2):
            term = dot(hid[M:R, :], ring[(LAST + n) % SLOTS, w])
            stage[n, :, w * T : (w + 1) * T] = term.astype(BF16)

    def own_rows(n):
        for w in range(2):
            keep[n % 6, :, w * T : (w + 1) * T] = dot(hid[O:M, :], ring[(LAST + n) % SLOTS, w])

    def arrived(n):
        arrive(LAST + n)

    each(arrived, 0, 1, 2, 3)
    send_sums(1, 1)
    each(mates_rows, 0, 1, 2, 3)
    each(own_rows, 0, 1, 2, 3)

    each(send_rows, 0, 1, 2, 3)
    each(arrived, 4, 5)
    each(mates_rows, 4, 5)
    each(own_rows, 4, 5)

    each(send_rows, 4, 5)
    each(take, 0, 1, 2, 3)
    each(arrived, 6, 7)
    each(total, 0, 1, 2, 3)
    each(mates_rows, 6, 7)

    each(send_rows, 6, 7)
    each(write_out, 0, 1, 2, 3)
    each(take, 4, 5)
    each(total, 4, 5)
    each(own_rows, 6, 7)

    each(write_out, 4, 5)
    each(take, 6, 7)
    each(total, 6, 7)
    each(write_out, 6, 7)

    for h in range(2):
        for n in range(DN):
            to_peer(h, n).wait_send()
    for n in range(DN):
        write(n).wait()


def move(y_ref, out_ref, buf, into, out):
    parts = range(4)
    rows = ROWS // len(parts)

    def load(i):
        return pltpu.make_async_copy(y_ref.at[pl.ds(i * rows, rows)], buf.at[i], into.at[i])

    def store(i):
        return pltpu.make_async_copy(buf.at[i], out_ref.at[pl.ds(i * rows, rows)], out.at[i])

    for i in parts:
        load(i).start()
    for i in parts:
        load(i).wait()
        store(i).start()
    for i in parts:
        store(i).wait()


def solution(mesh):
    def step(x, w_gate, w_up, w_down):
        dma = pltpu.SemaphoreType.DMA
        hbm = pl.BlockSpec(memory_space=pltpu.HBM)
        y = pl.pallas_call(
            kernel,
            out_shape=jax.ShapeDtypeStruct((ROWS, D), BF16),
            in_specs=[pl.BlockSpec(memory_space=pltpu.HBM)] * 4,
            out_specs=pl.BlockSpec(memory_space=pltpu.HBM),
            scratch_shapes=[
                pltpu.VMEM((4 * ROWS, D), BF16),
                pltpu.VMEM((3 * ROWS, D), BF16),
                pltpu.VMEM((SLOTS, 2, D, T), BF16),
                pltpu.VMEM((6, ROWS, W), F32),
                pltpu.VMEM((DN, ROWS, W), BF16),
                pltpu.VMEM((DN, HALF, W), BF16),
                pltpu.VMEM((DN, HALF, W), BF16),
                dma((SLOTS, 2)),
                dma,
                dma((DN,)),
                dma((5,)),
                dma((5,)),
                dma((2 * DN,)),
                dma((2 * DN,)),
                dma((2 * DN,)),
                dma((2 * DN,)),
                dma((DN,)),
                dma((DN,)),
                pltpu.SemaphoreType.REGULAR((2,)),
            ],
            compiler_params=pltpu.CompilerParams(
                collective_id=0, has_side_effects=True, vmem_limit_bytes=67043328
            ),
            name="mlp",
        )(x, w_gate, w_up, w_down)
        return pl.pallas_call(
            move,
            out_shape=jax.ShapeDtypeStruct((ROWS, D), BF16),
            in_specs=[hbm],
            out_specs=hbm,
            scratch_shapes=[pltpu.VMEM((4, ROWS // 4, D), BF16), dma((4,)), dma((4,))],
            name="move",
        )(y)

    return jax.shard_map(
        step,
        mesh=mesh,
        in_specs=(P(("dp", "tp"), None), P(None, "tp"), P(None, "tp"), P("tp", None)),
        out_specs=P(("dp", "tp"), None),
        check_vma=False,
    )
```

time: 270 us -> 122 us (0.45)
  matrix products: 131 us -> 0 us
  waiting for transfers between devices: 126 us -> 0 us
  Pallas kernels: 0 us -> 122 us
  between operations: 13.4 us -> 0.21 us
    dot_general x3 -> x0, matrix products: 131 us -> none  [the longest x1 45.1 us: step(): gate = jnp.dot(rows, w_gate, preferred_element_type=jnp.float32)]
    pallas_call x0 -> x2, Pallas kernels: none -> 122 us  [the longest x1 119 us: step(): pl.pallas_call(kernel, out_shape=jax.ShapeDtypeStruct((ROWS, D), BF16), i...]
    reduce_scatter x1 -> x0, waiting for transfers between devices: 65.3 us -> none  [step(): return lax.psum_scatter(term, 'tp', scatter_dimension=0, tiled=True)]
    all_gather x1 -> x0, waiting for transfers between devices: 60.1 us -> none  [step(): rows = lax.all_gather(x, 'tp', axis=0, tiled=True)]
  transfers between devices with their start and end apart: 2 -> 0, of which waited for: 2 -> 0; matrix products, arithmetic and copies ran while one was open for 0% -> 0% of each run, Pallas kernels for 0% -> 0%
where the time goes in v3:
time: 122 us
  Pallas kernels  122 us (100%)
    pallas_call x1, Pallas kernels, step(): pl.pallas_call(kernel, out_shape=jax.ShapeDtypeStruct((ROWS, D), BF16), i...  119 us

profile of v3, /device:TPU:0, one launch (start us, length us, event | category | flops | bytes accessed | tf_op | source)
XLA Modules:
  0.0 122.1 jit_solution(15998145260973754156)
XLA Ops:
  0.0 119.5 %mlp.1.y_ref = bf16[256,4096]{1,0:T(8,128)(2,1)} custom-call(bf16[256,4096]{1,0:T(8,128)(2,1)} %x_hbm.1, bf16[4096,4096]{1,0:T(8,128)(2,1)} %wg_hbm.1, bf16[4096,4096]{1,0:T(8,128)(2,1)} %wu_hbm.1, bf16[4096,4096]{1,0:T(8,128)(2,1)} %wd_hbm.1), custom_call_target="tpu_custom_call" | custom-call | tf_op jit(solution)/shard_map/mlp/pallas_call | solution.py:402
  119.5 2.4 %move.1 = bf16[256,4096]{1,0:T(8,128)(2,1)} custom-call(bf16[256,4096]{1,0:T(8,128)(2,1)} %mlp.1.y_ref), custom_call_target="tpu_custom_call" | custom-call | tf_op jit(solution)/shard_map/move/pallas_call | solution.py:433

commit v4 on v3

--- a/solution.py
+++ b/solution.py
@@ -27,9 +27,9 @@
 
 
 def kernel(
-    x_hbm, wg_hbm, wu_hbm, wd_hbm, y_hbm,
-    xv, hid, ring, keep, stage, drecv, yrecv,
-    wsem, xsem, osem, ag_send, ag_recv, d_send, d_recv, i_send, i_recv, p_send, p_recv, free,
+    x_hbm, wg_hbm, wu_hbm, wd_hbm, stage,
+    xv, hid, ring, keep, drecv, yrecv,
+    wsem, xsem, ag_send, ag_recv, d_send, d_recv, i_send, i_recv, p_send, p_recv, free,
 ):
     dp, tp = lax.axis_index("dp"), lax.axis_index("tp")
     chip, core = tp // 2, tp % 2
@@ -70,8 +70,8 @@
 
     own = pltpu.make_async_copy(x_hbm, xv.at[pl.ds(O, ROWS)], xsem)
     own.start()
-    fetch_gu(0, 0)
-    fetch_gu(1, 1)
+    for q in range(3):
+        fetch_gu(q, q)
     barrier = pltpu.get_barrier_semaphore()
     for to in (mate, peer):
         pl.semaphore_signal(barrier, inc=1, device_id=to, device_id_type=MESH)
@@ -93,14 +93,13 @@
 
     far(0).start()
     far(1).start()
-    for q in range(2, SLOTS):
-        fetch_gu(q, q)
     own.wait()
 
     def pass_own(q, _):
         arrive(q)
         gate_up(q, q, O, O)
-        fetch_gu(q + SLOTS, q + SLOTS)
+        for i in range(2):
+            fetch_gu(2 * q + 3 + i, 2 * q + 3 + i)
         return 0
 
     lax.fori_loop(0, LEFT, pass_own, 0)
@@ -112,11 +111,12 @@
         for i in range(u):
             gate_up(q + i, q + i, O, O)
             gate_up(q + i, q + i, M, M)
-        for i in range(u):
-            fetch_gu(q + i + SLOTS, lax.rem(q + i + SLOTS, LATE))
 
     def pass_single(q, _):
         pass_near(q, 1)
+        for i in range(3):
+            fetch_gu(3 * q + 1 + i, 3 * q + 1 + i)
+        pl.when(q == LEFT + 1)(lambda: fetch_gu(LATE - 1, LATE - 1))
         return 0
 
     lax.fori_loop(LEFT, LEFT + 2, pass_single, 0)
@@ -127,7 +127,10 @@
             far(0).wait_recv()
             forward(0).start()
 
-        pass_near(2 * j, 2)
+        q = 2 * j
+        pass_near(q, 2)
+        for i in range(2):
+            fetch_gu(q + i + SLOTS, lax.rem(q + i + SLOTS, LATE))
         return 0
 
     lax.fori_loop(LEFT // 2 + 1, LATE // 2, pass_double, 0)
@@ -145,7 +148,7 @@
     def to_mate(h, d, i):
         n = 4 * d + i
         k = h * DN + n
-        src = stage.at[2 * d + i // 2, pl.ds(i % 2 * HALF, HALF)]
+        src = stage.at[pl.ds(i % 2 * HALF, HALF), pl.ds((2 * d + i // 2) * W, W)]
         return remote(src, terms(h, n), d_send.at[k], d_recv.at[k], mate)
 
     def to_peer(h, n):
@@ -255,7 +258,8 @@
                     c = slice(w * T, (w + 1) * T)
                     term = dot(hid[R:, :], ring[slot, w])
                     keep[2 * d + i // 2, r, c] = term[:HALF]
-                    stage[2 * d + i // 2, r, c] = term[HALF:].astype(BF16)
+                    at = pl.multiple_of((2 * d + i // 2) * W + w * T, T)
+                    stage[r, pl.ds(at, T)] = term[HALF:].astype(BF16)
 
             @pl.when(h == 0)
             def _():
@@ -303,10 +307,8 @@
     combine(1, 1)
 
     def rows_to_mate(n):
-        return remote(stage.at[n], xv.at[pl.ds(R, ROWS), pl.ds(n * W, W)], p_send.at[n], p_recv.at[n], mate)
-
-    def write(n):
-        return pltpu.make_async_copy(stage.at[n], y_hbm.at[:, pl.ds(n * W, W)], osem.at[n])
+        c = pl.ds(n * W, W)
+        return remote(stage.at[:, c], xv.at[pl.ds(R, ROWS), c], p_send.at[n], p_recv.at[n], mate)
 
     def each(what, *steps):
         for n in steps:
@@ -325,15 +327,12 @@
             r = slice(h * HALF, (h + 1) * HALF)
             mates = xv[R + h * HALF : R + (h + 1) * HALF, n * W : (n + 1) * W].astype(F32)
             y = keep[n % 6, r] + mates + sums(h, n)[...].astype(F32)
-            stage[n, r] = y.astype(BF16)
-
-    def write_out(n):
-        write(n).start()
+            stage[r, n * W : (n + 1) * W] = y.astype(BF16)
 
     def mates_rows(n):
         for w in range(2):
             term = dot(hid[M:R, :], ring[(LAST + n) % SLOTS, w])
-            stage[n, :, w * T : (w + 1) * T] = term.astype(BF16)
+            stage[:, n * W + w * T : n * W + (w + 1) * T] = term.astype(BF16)
 
     def own_rows(n):
         for w in range(2):
@@ -359,62 +358,36 @@
     each(mates_rows, 6, 7)
 
     each(send_rows, 6, 7)
-    each(write_out, 0, 1, 2, 3)
     each(take, 4, 5)
     each(total, 4, 5)
     each(own_rows, 6, 7)
 
-    each(write_out, 4, 5)
     each(take, 6, 7)
     each(total, 6, 7)
-    each(write_out, 6, 7)
 
     for h in range(2):
         for n in range(DN):
             to_peer(h, n).wait_send()
-    for n in range(DN):
-        write(n).wait()
-
-
-def move(y_ref, out_ref, buf, into, out):
-    parts = range(4)
-    rows = ROWS // len(parts)
-
-    def load(i):
-        return pltpu.make_async_copy(y_ref.at[pl.ds(i * rows, rows)], buf.at[i], into.at[i])
-
-    def store(i):
-        return pltpu.make_async_copy(buf.at[i], out_ref.at[pl.ds(i * rows, rows)], out.at[i])
-
-    for i in parts:
-        load(i).start()
-    for i in parts:
-        load(i).wait()
-        store(i).start()
-    for i in parts:
-        store(i).wait()
 
 
 def solution(mesh):
     def step(x, w_gate, w_up, w_down):
         dma = pltpu.SemaphoreType.DMA
         hbm = pl.BlockSpec(memory_space=pltpu.HBM)
-        y = pl.pallas_call(
+        return pl.pallas_call(
             kernel,
-            out_shape=jax.ShapeDtypeStruct((ROWS, D), BF16),
-            in_specs=[pl.BlockSpec(memory_space=pltpu.HBM)] * 4,
-            out_specs=pl.BlockSpec(memory_space=pltpu.HBM),
+            out_shape=pltpu.VMEM((ROWS, D), BF16),
+            in_specs=[hbm] * 4,
+            out_specs=pl.BlockSpec(memory_space=pltpu.VMEM),
             scratch_shapes=[
                 pltpu.VMEM((4 * ROWS, D), BF16),
                 pltpu.VMEM((3 * ROWS, D), BF16),
                 pltpu.VMEM((SLOTS, 2, D, T), BF16),
                 pltpu.VMEM((6, ROWS, W), F32),
-                pltpu.VMEM((DN, ROWS, W), BF16),
                 pltpu.VMEM((DN, HALF, W), BF16),
                 pltpu.VMEM((DN, HALF, W), BF16),
                 dma((SLOTS, 2)),
                 dma,
-                dma((DN,)),
                 dma((5,)),
                 dma((5,)),
                 dma((2 * DN,)),
@@ -426,18 +399,10 @@
                 pltpu.SemaphoreType.REGULAR((2,)),
             ],
             compiler_params=pltpu.CompilerParams(
-                collective_id=0, has_side_effects=True, vmem_limit_bytes=67043328
+                collective_id=0, has_side_effects=True, vmem_limit_bytes=123 * 2**19
             ),
             name="mlp",
         )(x, w_gate, w_up, w_down)
-        return pl.pallas_call(
-            move,
-            out_shape=jax.ShapeDtypeStruct((ROWS, D), BF16),
-            in_specs=[hbm],
-            out_specs=hbm,
-            scratch_shapes=[pltpu.VMEM((4, ROWS // 4, D), BF16), dma((4,)), dma((4,))],
-            name="move",
-        )(y)
 
     return jax.shard_map(
         step,

time: 122 us -> 121 us (level)
  Pallas kernels: 122 us -> 119 us
  local copies, waits for them, and re-layouts: 0 us -> 1.32 us
    pallas_call x2 -> x1, Pallas kernels: 122 us -> 119 us  [step(): pl.pallas_call(kernel, out_shape=pltpu.VMEM((ROWS, D), BF16), in_specs=[h...]
    unnamed x0 -> x1, local copies, waits for them, and re-layouts: none -> 1.32 us
where the time goes in v4:
time: 121 us
  Pallas kernels  119 us (98%)
  local copies, waits for them, and re-layouts  1.32 us (1%)
    pallas_call x1, Pallas kernels, step(): pl.pallas_call(kernel, out_shape=pltpu.VMEM((ROWS, D), BF16), in_specs=[h...  119 us

profile of v4, /device:TPU:0, one launch (start us, length us, event | category | flops | bytes accessed | tf_op | source)
XLA Modules:
  0.0 120.8 jit_solution(7647473113122360070)
XLA Ops:
  0.0 119.4 %mlp.1 = bf16[256,4096]{1,0:T(8,128)(2,1)S(1)} custom-call(bf16[256,4096]{1,0:T(8,128)(2,1)} %x_hbm.1, bf16[4096,4096]{1,0:T(8,128)(2,1)} %wg_hbm.1, bf16[4096,4096]{1,0:T(8,128)(2,1)} %wu_hbm.1, bf16[4096,4096]{1,0:T(8,128)(2,1)} %wd_hbm.1), custom_call_target="tpu_custom_call" | custom-call | tf_op jit(solution)/shard_map/mlp/pallas_call | solution.py:377
  119.5 1.3 %copy.6 = bf16[256,4096]{1,0:T(8,128)(2,1)} copy(bf16[256,4096]{1,0:T(8,128)(2,1)S(1)} %mlp.1) | data formatting | bytes 4194304

commit v5 on v4

--- a/solution.py
+++ b/solution.py
@@ -70,7 +70,7 @@
 
     own = pltpu.make_async_copy(x_hbm, xv.at[pl.ds(O, ROWS)], xsem)
     own.start()
-    for q in range(3):
+    for q in range(2):
         fetch_gu(q, q)
     barrier = pltpu.get_barrier_semaphore()
     for to in (mate, peer):
@@ -93,13 +93,14 @@
 
     far(0).start()
     far(1).start()
+    for q in range(2, SLOTS):
+        fetch_gu(q, q)
     own.wait()
 
     def pass_own(q, _):
         arrive(q)
         gate_up(q, q, O, O)
-        for i in range(2):
-            fetch_gu(2 * q + 3 + i, 2 * q + 3 + i)
+        fetch_gu(q + SLOTS, q + SLOTS)
         return 0
 
     lax.fori_loop(0, LEFT, pass_own, 0)
@@ -114,9 +115,7 @@
 
     def pass_single(q, _):
         pass_near(q, 1)
-        for i in range(3):
-            fetch_gu(3 * q + 1 + i, 3 * q + 1 + i)
-        pl.when(q == LEFT + 1)(lambda: fetch_gu(LATE - 1, LATE - 1))
+        fetch_gu(q + SLOTS, q + SLOTS)
         return 0
 
     lax.fori_loop(LEFT, LEFT + 2, pass_single, 0)

time: 121 us -> 120 us (level)
  no operation moved by 1% of the time
where the time goes in v5:
time: 120 us
  Pallas kernels  119 us (99%)
  local copies, waits for them, and re-layouts  1.32 us (1%)
    pallas_call x1, Pallas kernels, step(): pl.pallas_call(kernel, out_shape=pltpu.VMEM((ROWS, D), BF16), in_specs=[h...  119 us

profile of v5, /device:TPU:0, one launch (start us, length us, event | category | flops | bytes accessed | tf_op | source)
XLA Modules:
  0.0 119.9 jit_solution(1136734726221937499)
XLA Ops:
  0.0 118.6 %mlp.1 = bf16[256,4096]{1,0:T(8,128)(2,1)S(1)} custom-call(bf16[256,4096]{1,0:T(8,128)(2,1)} %x_hbm.1, bf16[4096,4096]{1,0:T(8,128)(2,1)} %wg_hbm.1, bf16[4096,4096]{1,0:T(8,128)(2,1)} %wu_hbm.1, bf16[4096,4096]{1,0:T(8,128)(2,1)} %wd_hbm.1), custom_call_target="tpu_custom_call" | custom-call | tf_op jit(solution)/shard_map/mlp/pallas_call | solution.py:376
  118.6 1.3 %copy.6 = bf16[256,4096]{1,0:T(8,128)(2,1)} copy(bf16[256,4096]{1,0:T(8,128)(2,1)S(1)} %mlp.1) | data formatting | bytes 4194304
